TPU v7x, 32 devices: a whole 2x2x4 slice. The times are simulated.
32 devices in a mesh: node: 8 (over z, x), rep: 4 (over y, core).
Axes of the slice: x: 2, y: 2, z: 4, core: 2. Of those that a mesh axis runs over, the one named last changes fastest.
Arguments:
- features: bfloat16 [163840, 256], P('node'), may hold values from -6 to 6
- w_in: bfloat16 [256, 256], replicated, may hold values from -0.375 to 0.375
- w_out: bfloat16 [256, 256], replicated, may hold values from -0.375 to 0.375
- pos_src: int32 [8, 4, 8, 2], P('node', 'rep'), may hold values from 0 to 159
- pos_dst: int32 [8, 4, 8, 2], P('node', 'rep'), may hold values from 0 to 159
- counts: int32 [8, 4, 8], P('node', 'rep'), may hold values from 1 to 2, as said below
- neg_blocks: int32 [8, 2], P('node'), may hold values from 0 to 159
- neg_pick: int32 [8, 4, 8, 2], P('node', 'rep'), may hold values from 0 to 15
Outputs:
- pos_scores: float32 [8, 4, 8, 2, 128], P('node', 'rep')
- neg_term: float32 [8, 4, 8, 2, 128], P('node', 'rep')
- loss: float32 [], replicated
Inputs may be any that keep to these rules, and one draw needn't show every extreme that they name: `counts`: each entry is at most 2; in every draw one owner receives 2 live slots from every device.
All inputs are finite; a program needn't handle non-finite values.
Results may differ from a plain program's by a relative error of at most 0.0027.
Values may be sent and summed in bfloat16 or wider, within the bound.
A program may use at most 192 MiB of HBM per device.

v0:
```python
import jax
import jax.numpy as jnp
from jax import lax
from jax.sharding import PartitionSpec as P

BLK = 128


def encode(rows_in, w_in, w_out):
    hidden = jax.nn.silu(jnp.dot(rows_in, w_in, preferred_element_type=jnp.float32)).astype(
        jnp.bfloat16
    )
    return jnp.dot(hidden, w_out, preferred_element_type=jnp.float32).astype(jnp.bfloat16)


def shards(features, w_in, w_out, pos_src, pos_dst, counts, neg_blocks, neg_pick):
    rows, width = features.shape
    owners = pos_dst.shape[2]
    slots = pos_dst.shape[3]
    embed = encode(features, w_in, w_out)
    blocks = embed.reshape(rows // BLK, BLK, width)
    asked_ids = pos_dst.reshape(owners, slots)
    reply = jnp.take(
        blocks, lax.all_to_all(asked_ids, "node", split_axis=0, concat_axis=0, tiled=True), axis=0
    )
    fetched = lax.all_to_all(reply, "node", split_axis=0, concat_axis=0, tiled=True)
    offered = jnp.take(blocks, neg_blocks.reshape(-1), axis=0)
    pool = lax.all_gather(offered, "node", axis=0, tiled=True)
    source = jnp.take(blocks, pos_src.reshape(-1), axis=0).reshape(owners, slots, BLK, width)
    cand = jnp.take(pool, neg_pick.reshape(-1), axis=0).reshape(owners, slots, BLK, width)
    scale = 1.0 / width**0.5
    raw_pos = (
        jnp.einsum("ocbd,ocbd->ocb", source, fetched, preferred_element_type=jnp.float32) * scale
    )
    scores = jnp.einsum("ocbd,ocsd->ocbs", source, cand, preferred_element_type=jnp.float32) * scale
    live = jnp.arange(slots, dtype=jnp.int32)[None, :] < counts.reshape(owners, 1)
    livex = live[..., None]
    pos_out = jnp.where(livex, raw_pos, 0.0)
    neg_out = jnp.where(livex, jnp.mean(jax.nn.softplus(scores), axis=-1), 0.0)
    pos_loss = jnp.sum(jnp.where(livex, jax.nn.softplus(-raw_pos), 0.0))
    totals = lax.psum(
        (pos_loss, jnp.sum(neg_out), jnp.sum(counts).astype(jnp.float32)), ("node", "rep")
    )
    loss = (totals[0] + totals[1]) / (BLK * totals[2])
    return (
        pos_out.reshape(1, 1, owners, slots, BLK),
        neg_out.reshape(1, 1, owners, slots, BLK),
        loss,
    )


def solution(mesh):
    return jax.shard_map(
        shards,
        mesh=mesh,
        in_specs=(
            P("node", None),
            P(),
            P(),
            P("node", "rep", None, None),
            P("node", "rep", None, None),
            P("node", "rep", None),
            P("node", None),
            P("node", "rep", None, None),
        ),
        out_specs=(P("node", "rep", None, None, None), P("node", "rep", None, None, None), P()),
        check_vma=False,
    )
```

profile of v0, /device:TPU:0, one launch (start us, length us, event | category | flops | bytes accessed | tf_op | source)
XLA Modules:
  0.0 137.5 jit_solution(16845520026060009428)
XLA Ops:
  7.2 0.0 copy-start
  7.2 1.4 %copy.25 = s32[8,1,2]{2,1,0:T(1,128)} copy(s32[8,1,2]{0,2,1:T(2,128)} %bitcast.44) | data formatting | bytes 128 | tf_op jit(solution)/shard_map/all_to_all | solution.py:24
  8.6 7.3 %all-to-all-start = ((s32[8,1,2]{2,1,0:T(1,128)}), s32[8,1,2]{2,1,0:T(1,128)S(1)}, u32[]{:S(2)}, u32[]{:S(2)}) async-start(s32[8,1,2]{2,1,0:T(1,128)} %copy.25), calls=%async_computation | async-start | bytes 8192 | tf_op jit(solution)/shard_map/all_to_all | solution.py:24
  15.8 0.0 all-gather.2.cloned.1.call-start
  15.9 0.7 fusion.8
  16.5 0.7 compare_and_fusion
  17.2 0.0 copy-done
  17.2 0.0 copy-start.3
  17.2 0.0 copy-start.1
  17.2 0.0 copy-start.2
  17.3 10.9 %convolution_convert_fusion = bf16[20480,256]{1,0:T(8,128)(2,1)} fusion(bf16[256,256]{1,0:T(8,128)(2,1)S(1)} %copy-done, bf16[20480,256]{1,0:T(8,128)(2,1)} %param.8, bf16[256,256]{1,0:T(8,128)(2,1)} %param.9), kind=kOutput, calls=%fused_computation.4 | convolution fusion | flops 5400166400 | bytes 21233664 | tf_op jit(solution)/shard_map/dot_general | solution.py:13
  28.2 4.5 %gather_fusion.2 = bf16[2,128,256]{2,1,0:T(8,128)(2,1)S(1)} fusion(bf16[160,128,256]{2,1,0:T(8,128)(2,1)} %bitcast.41, s32[1024]{0:T(1024)S(1)} %pad_clamp_fusion.1), kind=kCustom, calls=%fused_computation.2 | custom fusion | bytes 262152 | tf_op jit(solution)/shard_map/jit(_take)/gather | solution.py:27
  32.7 0.7 broadcast_select_fusion.3
  33.5 0.0 all-gather.2.cloned.1.call-update
  33.5 0.0 copy-done.3
  33.5 0.6 reduce_sum.39
  34.8 0.0 copy-done.1
  34.8 0.1 copy.24
  34.9 0.0 all-to-all-done
  34.9 0.1 copy.26
  35.0 0.1 copy.27
  35.1 0.1 copy.29
  35.1 0.1 reshape.231
  35.2 4.6 %gather_fusion.1 = bf16[16,128,256]{2,1,0:T(8,128)(2,1)S(1)} fusion(bf16[160,128,256]{2,1,0:T(8,128)(2,1)} %bitcast.42, s32[1024]{0:T(1024)S(1)} %pad_clamp_fusion.2), kind=kCustom, calls=%fused_computation.1 | custom fusion | bytes 2097216 | tf_op jit(solution)/shard_map/jit(_take)/gather | solution.py:23
  39.8 1.1 broadcast_select_fusion
  41.0 6.0 %all-to-all-start.1 = ((bf16[8,2,128,256]{3,2,1,0:T(8,128)(2,1)}), bf16[8,2,128,256]{3,2,1,0:T(8,128)(2,1)S(1)}, u32[]{:S(2)}, u32[]{:S(2)}) async-start(bf16[8,2,128,256]{3,2,1,0:T(8,128)(2,1)} %broadcast_select_fusion), calls=%async_computation.1 | async-start | bytes 2097152 | tf_op jit(solution)/shard_map/all_to_all | solution.py:26
  46.9 0.1 copy.23
  47.0 0.0 copy-done.2
  47.0 0.1 copy.31
  47.1 0.1 copy.30
  47.2 0.1 reshape.215
  47.3 0.1 reshape.220
  47.4 4.6 %gather_fusion = bf16[16,128,256]{2,1,0:T(8,128)(2,1)S(1)} fusion(bf16[160,128,256]{2,1,0:T(8,128)(2,1)} %bitcast.43, s32[1024]{0:T(1024)S(1)} %pad_clamp_fusion.3), kind=kCustom, calls=%fused_computation | custom fusion | bytes 2097216 | tf_op jit(solution)/shard_map/jit(_take)/gather | solution.py:29
  52.0 0.1 iota_compare_fusion
  52.1 30.7 %all-gather.2.cloned.1.call-done = bf16[16,128,256]{2,1,0:T(8,128)(2,1)} async-done(((bf16[2,128,256]{2,1,0:T(8,128)(2,1)}), bf16[16,128,256]{2,1,0:T(8,128)(2,1)}) %all-gather.2.cloned.1.call-update) | async-done | bytes 1048592 | tf_op jit(solution)/shard_map/all_gather | solution.py:28
  82.8 1.8 %gather_fusion.3 = bf16[16,128,256]{2,1,0:T(8,128)(2,1)S(1)} fusion(bf16[16,128,256]{2,1,0:T(8,128)(2,1)} %all-gather.2.cloned.1.call-done, s32[1024]{0:T(1024)S(1)} %pad_clamp_fusion), kind=kCustom, calls=%fused_computation.3 | custom fusion | bytes 2097216 | tf_op jit(solution)/shard_map/jit(_take)/gather | solution.py:30
  84.7 0.5 fusion.4
  85.2 0.6 select_reduce_fusion
  85.9 0.0 all-to-all-done.1
  85.9 0.5 fusion
  86.4 1.3 select_reduce_fusion.1
  89.0 0.7 bitcast_select_fusion
  89.7 38.6 %all-reduce = (f32[]{:T(128)}, f32[]{:T(128)}) all-reduce(f32[]{:T(128)S(6)} %add.94, f32[]{:T(128)S(6)} %convert_element_type.11), channel_id=1, replica_groups=mesh['node'=8,'rep'=4] {'node','rep'}, use_global_device_ids=true, to_apply=%region_2.3 | all-reduce | flops 2 | bytes 16 | tf_op jit(solution)/shard_map/psum | solution.py:41
  (10 shorter events, 0.1 us)
Async XLA Ops:
  7.2 10.1 %copy-start = (bf16[256,256]{1,0:T(8,128)(2,1)S(1)}, bf16[256,256]{1,0:T(8,128)(2,1)}, u32[]{:S(2)}) copy-start(bf16[256,256]{1,0:T(8,128)(2,1)} %param.10) | copy-start | bytes 393220
  8.6 26.3 %all-to-all-start = ((s32[8,1,2]{2,1,0:T(1,128)}), s32[8,1,2]{2,1,0:T(1,128)S(1)}, u32[]{:S(2)}, u32[]{:S(2)}) async-start(s32[8,1,2]{2,1,0:T(1,128)} %copy.25), calls=%async_computation | async-start | bytes 8192 | tf_op jit(solution)/shard_map/all_to_all | solution.py:24
  15.8 67.0 %all-gather.2.cloned.1.call-start = ((), (), s32[]{:S(2)}) async-start(), calls=%async_computation.2 | async-start | bytes 1179648 | tf_op jit(solution)/shard_map/all_gather | solution.py:28
  17.2 16.3 %copy-start.3 = (s32[1,1,8]{2,1,0:T(1,128)S(1)}, s32[1,1,8]{2,1,0:T(1,128)}, u32[]{:S(2)}) copy-start(s32[1,1,8]{2,1,0:T(1,128)} %param.13) | copy-start | bytes 100
  17.2 17.5 %copy-start.1 = (s32[1,1,8,2]{2,3,1,0:T(2,128)S(1)}, s32[1,1,8,2]{2,3,1,0:T(2,128)}, u32[]{:S(2)}) copy-start(s32[1,1,8,2]{2,3,1,0:T(2,128)} %param.11) | copy-start | bytes 196
  17.2 29.8 %copy-start.2 = (s32[1,1,8,2]{2,3,1,0:T(2,128)S(1)}, s32[1,1,8,2]{2,3,1,0:T(2,128)}, u32[]{:S(2)}) copy-start(s32[1,1,8,2]{2,3,1,0:T(2,128)} %param.15) | copy-start | bytes 196
  41.0 44.9 %all-to-all-start.1 = ((bf16[8,2,128,256]{3,2,1,0:T(8,128)(2,1)}), bf16[8,2,128,256]{3,2,1,0:T(8,128)(2,1)S(1)}, u32[]{:S(2)}, u32[]{:S(2)}) async-start(bf16[8,2,128,256]{3,2,1,0:T(8,128)(2,1)} %broadcast_select_fusion), calls=%async_computation.1 | async-start | bytes 2097152 | tf_op jit(solution)/shard_map/all_to_all | solution.py:26
Sparse Core Ops, SparseCore 0:
  33.6 49.2 all-gather.1
where the time goes:
time: 138 us
  blocking collectives  38.6 us (28%)
  waiting for transfers between devices  30.7 us (22%)
  between operations  18.6 us (13%)
  local copies, waits for them, and re-layouts  17.8 us (13%)
  starting transfers between devices  13.3 us (10%)
  matrix products  11.5 us (8%)
  other arithmetic  7.07 us (5%)
    psum x1, blocking collectives, shards(): lax.psum((pos_loss, jnp.sum(neg_out), jnp.sum(counts).astype(jnp.float32)...  38.6 us
    all_gather x1, waiting for transfers between devices, shards(): pool = lax.all_gather(offered, 'node', axis=0, tiled=True)  30.7 us
    dot_general x1, matrix products, encode(): jnp.dot(hidden, w_out, preferred_element_type=jnp.float32)  10.9 us
    all_to_all x1, starting transfers between devices, shards(): lax.all_to_all(asked_ids, 'node', split_axis=0, concat_axis=0, tiled=True)  7.28 us
    all_to_all x1, starting transfers between devices, shards(): lax.all_to_all(reply, 'node', split_axis=0, concat_axis=0, tiled=True)  5.95 us
    gather x1, local copies, waits for them, and re-layouts, shards(): jnp.take(blocks, pos_src.reshape(-1), axis=0)  4.61 us
    gather x1, local copies, waits for them, and re-layouts, shards(): jnp.take(blocks, lax.all_to_all(asked_ids, 'node', split_axis=0, concat_a...  4.59 us
    gather x1, local copies, waits for them, and re-layouts, shards(): offered = jnp.take(blocks, neg_blocks.reshape(-1), axis=0)  4.53 us
  transfers between devices with their start and end apart: 3, of which 1 were waited for; matrix products, arithmetic and copies ran while one was open for 24% of the time, Pallas kernels for 0%

commit v1 on v0

--- a/solution.py
+++ b/solution.py
@@ -39,7 +39,7 @@
     neg_out = jnp.where(livex, jnp.mean(jax.nn.softplus(scores), axis=-1), 0.0)
     pos_loss = jnp.sum(jnp.where(livex, jax.nn.softplus(-raw_pos), 0.0))
     totals = lax.psum(
-        (pos_loss, jnp.sum(neg_out), jnp.sum(counts).astype(jnp.float32)), ("node", "rep")
+        lax.psum((pos_loss, jnp.sum(neg_out), jnp.sum(counts).astype(jnp.float32)), "rep"), "node"
     )
     loss = (totals[0] + totals[1]) / (BLK * totals[2])
     return (

time: 138 us -> 126 us (0.913)
  blocking collectives: 38.6 us -> 26.8 us
    psum x1, blocking collectives: 38.6 us -> 7.43 us  [shards(): lax.psum((pos_loss, jnp.sum(neg_out), jnp.sum(counts).astype(jnp.float32)...]
    psum x0 -> x1, blocking collectives: none -> 19.4 us  [shards(): lax.psum(lax.psum((pos_loss, jnp.sum(neg_out), jnp.sum(counts).astype(jnp...]
  transfers between devices with their start and end apart: 3 -> 3, of which waited for: 1 -> 1; matrix products, arithmetic and copies ran while one was open for 24% -> 26% of each run, Pallas kernels for 0% -> 0%
where the time goes in v1:
time: 126 us
  waiting for transfers between devices  30.7 us (24%)
  blocking collectives  26.8 us (21%)
  between operations  18.5 us (15%)
  local copies, waits for them, and re-layouts  17.8 us (14%)
  starting transfers between devices  13.3 us (11%)
  matrix products  11.5 us (9%)
  other arithmetic  7.07 us (6%)
    all_gather x1, waiting for transfers between devices, shards(): pool = lax.all_gather(offered, 'node', axis=0, tiled=True)  30.7 us
    psum x1, blocking collectives, shards(): lax.psum(lax.psum((pos_loss, jnp.sum(neg_out), jnp.sum(counts).astype(jnp...  19.4 us
    dot_general x1, matrix products, encode(): jnp.dot(hidden, w_out, preferred_element_type=jnp.float32)  10.9 us
    psum x1, blocking collectives, shards(): lax.psum((pos_loss, jnp.sum(neg_out), jnp.sum(counts).astype(jnp.float32)...  7.43 us
    all_to_all x1, starting transfers between devices, shards(): lax.all_to_all(asked_ids, 'node', split_axis=0, concat_axis=0, tiled=True)  7.28 us
    all_to_all x1, starting transfers between devices, shards(): lax.all_to_all(reply, 'node', split_axis=0, concat_axis=0, tiled=True)  5.95 us
    gather x1, local copies, waits for them, and re-layouts, shards(): jnp.take(blocks, pos_src.reshape(-1), axis=0)  4.61 us
    gather x1, local copies, waits for them, and re-layouts, shards(): jnp.take(blocks, lax.all_to_all(asked_ids, 'node', split_axis=0, concat_a...  4.59 us
  transfers between devices with their start and end apart: 3, of which 1 were waited for; matrix products, arithmetic and copies ran while one was open for 26% of the time, Pallas kernels for 0%

profile of v1, /device:TPU:0, one launch (start us, length us, event | category | flops | bytes accessed | tf_op | source)
XLA Modules:
  0.0 125.6 jit_solution(13070972603221846196)
XLA Ops:
  7.2 0.0 copy-start
  7.2 1.4 %copy.25 = s32[8,1,2]{2,1,0:T(1,128)} copy(s32[8,1,2]{0,2,1:T(2,128)} %bitcast.44) | data formatting | bytes 128 | tf_op jit(solution)/shard_map/all_to_all | solution.py:24
  8.6 7.3 %all-to-all-start = ((s32[8,1,2]{2,1,0:T(1,128)}), s32[8,1,2]{2,1,0:T(1,128)S(1)}, u32[]{:S(2)}, u32[]{:S(2)}) async-start(s32[8,1,2]{2,1,0:T(1,128)} %copy.25), calls=%async_computation | async-start | bytes 8192 | tf_op jit(solution)/shard_map/all_to_all | solution.py:24
  15.8 0.0 all-gather.2.cloned.1.call-start
  15.9 0.7 fusion.8
  16.5 0.7 compare_and_fusion
  17.2 0.0 copy-done
  17.2 0.0 copy-start.3
  17.2 0.0 copy-start.1
  17.2 0.0 copy-start.2
  17.3 10.9 %convolution_convert_fusion = bf16[20480,256]{1,0:T(8,128)(2,1)} fusion(bf16[256,256]{1,0:T(8,128)(2,1)S(1)} %copy-done, bf16[20480,256]{1,0:T(8,128)(2,1)} %param.8, bf16[256,256]{1,0:T(8,128)(2,1)} %param.9), kind=kOutput, calls=%fused_computation.4 | convolution fusion | flops 5400166400 | bytes 21233664 | tf_op jit(solution)/shard_map/dot_general | solution.py:13
  28.2 4.5 %gather_fusion.2 = bf16[2,128,256]{2,1,0:T(8,128)(2,1)S(1)} fusion(bf16[160,128,256]{2,1,0:T(8,128)(2,1)} %bitcast.41, s32[1024]{0:T(1024)S(1)} %pad_clamp_fusion.1), kind=kCustom, calls=%fused_computation.2 | custom fusion | bytes 262152 | tf_op jit(solution)/shard_map/jit(_take)/gather | solution.py:27
  32.7 0.7 broadcast_select_fusion.3
  33.5 0.0 all-gather.2.cloned.1.call-update
  33.5 0.0 copy-done.3
  33.5 0.6 reduce_sum.39
  34.8 0.0 copy-done.1
  34.8 0.1 copy.24
  34.9 0.0 all-to-all-done
  34.9 0.1 copy.26
  35.0 0.1 copy.27
  35.1 0.1 copy.29
  35.1 0.1 reshape.231
  35.2 4.6 %gather_fusion.1 = bf16[16,128,256]{2,1,0:T(8,128)(2,1)S(1)} fusion(bf16[160,128,256]{2,1,0:T(8,128)(2,1)} %bitcast.42, s32[1024]{0:T(1024)S(1)} %pad_clamp_fusion.2), kind=kCustom, calls=%fused_computation.1 | custom fusion | bytes 2097216 | tf_op jit(solution)/shard_map/jit(_take)/gather | solution.py:23
  39.8 1.1 broadcast_select_fusion
  41.0 6.0 %all-to-all-start.1 = ((bf16[8,2,128,256]{3,2,1,0:T(8,128)(2,1)}), bf16[8,2,128,256]{3,2,1,0:T(8,128)(2,1)S(1)}, u32[]{:S(2)}, u32[]{:S(2)}) async-start(bf16[8,2,128,256]{3,2,1,0:T(8,128)(2,1)} %broadcast_select_fusion), calls=%async_computation.1 | async-start | bytes 2097152 | tf_op jit(solution)/shard_map/all_to_all | solution.py:26
  46.9 0.1 copy.23
  47.0 0.0 copy-done.2
  47.0 0.1 copy.31
  47.1 0.1 copy.30
  47.2 0.1 reshape.215
  47.3 0.1 reshape.220
  47.4 4.6 %gather_fusion = bf16[16,128,256]{2,1,0:T(8,128)(2,1)S(1)} fusion(bf16[160,128,256]{2,1,0:T(8,128)(2,1)} %bitcast.43, s32[1024]{0:T(1024)S(1)} %pad_clamp_fusion.3), kind=kCustom, calls=%fused_computation | custom fusion | bytes 2097216 | tf_op jit(solution)/shard_map/jit(_take)/gather | solution.py:29
  52.0 0.1 iota_compare_fusion
  52.1 30.7 %all-gather.2.cloned.1.call-done = bf16[16,128,256]{2,1,0:T(8,128)(2,1)} async-done(((bf16[2,128,256]{2,1,0:T(8,128)(2,1)}), bf16[16,128,256]{2,1,0:T(8,128)(2,1)}) %all-gather.2.cloned.1.call-update) | async-done | bytes 1048592 | tf_op jit(solution)/shard_map/all_gather | solution.py:28
  82.8 1.8 %gather_fusion.3 = bf16[16,128,256]{2,1,0:T(8,128)(2,1)S(1)} fusion(bf16[16,128,256]{2,1,0:T(8,128)(2,1)} %all-gather.2.cloned.1.call-done, s32[1024]{0:T(1024)S(1)} %pad_clamp_fusion), kind=kCustom, calls=%fused_computation.3 | custom fusion | bytes 2097216 | tf_op jit(solution)/shard_map/jit(_take)/gather | solution.py:30
  84.7 0.5 fusion.4
  85.2 0.6 select_reduce_fusion
  85.9 0.0 all-to-all-done.1
  85.9 0.5 fusion
  86.4 1.3 %select_reduce_fusion.1 = (f32[]{:T(128)}, f32[]{:T(128)}, f32[1,1,8,2,128]{4,3,2,1,0:T(2,128)}) fusion(pred[8,2]{1,0:T(8,128)(4,1)S(1)} %iota_compare_fusion, f32[8,2,128]{2,1,0:T(2,128)S(1)} %select_reduce_fusion, f32[8,2,128]{2,1,0:T(2,128)S(1)} %fusion), kind=kLoop, calls=%fused_computation.22 | loop fusion | flops 28670 | bytes 24600 | tf_op jit(solution)/shard_map/reduce_sum | solution.py:42
  89.0 0.7 bitcast_select_fusion
  89.7 7.4 %all-reduce.1 = (f32[]{:T(128)}, f32[]{:T(128)}) all-reduce(f32[]{:T(128)S(6)} %add.100, f32[]{:T(128)S(6)} %convert_element_type.11), channel_id=1, replica_groups=mesh['node'=8,'rep'=4] {'rep'}, use_global_device_ids=true, to_apply=%region_2.3 | all-reduce | flops 2 | bytes 16 | tf_op jit(solution)/shard_map/psum | solution.py:42
  97.1 19.4 %all-reduce = (f32[]{:T(128)}, f32[]{:T(128)}) all-reduce(f32[]{:T(128)} %get-tuple-element.7, f32[]{:T(128)} %get-tuple-element.8), channel_id=1, replica_groups=mesh['node'=8,'rep'=4] {'node'}, use_global_device_ids=true, to_apply=%region_3.4 | all-reduce | flops 2 | bytes 16 | tf_op jit(solution)/shard_map/psum | solution.py:41
  (10 shorter events, 0.1 us)
Async XLA Ops:
  7.2 10.1 %copy-start = (bf16[256,256]{1,0:T(8,128)(2,1)S(1)}, bf16[256,256]{1,0:T(8,128)(2,1)}, u32[]{:S(2)}) copy-start(bf16[256,256]{1,0:T(8,128)(2,1)} %param.10) | copy-start | bytes 393220
  8.6 26.3 %all-to-all-start = ((s32[8,1,2]{2,1,0:T(1,128)}), s32[8,1,2]{2,1,0:T(1,128)S(1)}, u32[]{:S(2)}, u32[]{:S(2)}) async-start(s32[8,1,2]{2,1,0:T(1,128)} %copy.25), calls=%async_computation | async-start | bytes 8192 | tf_op jit(solution)/shard_map/all_to_all | solution.py:24
  15.8 67.0 %all-gather.2.cloned.1.call-start = ((), (), s32[]{:S(2)}) async-start(), calls=%async_computation.2 | async-start | bytes 1179648 | tf_op jit(solution)/shard_map/all_gather | solution.py:28
  17.2 16.3 %copy-start.3 = (s32[1,1,8]{2,1,0:T(1,128)S(1)}, s32[1,1,8]{2,1,0:T(1,128)}, u32[]{:S(2)}) copy-start(s32[1,1,8]{2,1,0:T(1,128)} %param.13) | copy-start | bytes 100
  17.2 17.5 %copy-start.1 = (s32[1,1,8,2]{2,3,1,0:T(2,128)S(1)}, s32[1,1,8,2]{2,3,1,0:T(2,128)}, u32[]{:S(2)}) copy-start(s32[1,1,8,2]{2,3,1,0:T(2,128)} %param.11) | copy-start | bytes 196
  17.2 29.8 %copy-start.2 = (s32[1,1,8,2]{2,3,1,0:T(2,128)S(1)}, s32[1,1,8,2]{2,3,1,0:T(2,128)}, u32[]{:S(2)}) copy-start(s32[1,1,8,2]{2,3,1,0:T(2,128)} %param.15) | copy-start | bytes 196
  41.0 44.9 %all-to-all-start.1 = ((bf16[8,2,128,256]{3,2,1,0:T(8,128)(2,1)}), bf16[8,2,128,256]{3,2,1,0:T(8,128)(2,1)S(1)}, u32[]{:S(2)}, u32[]{:S(2)}) async-start(bf16[8,2,128,256]{3,2,1,0:T(8,128)(2,1)} %broadcast_select_fusion), calls=%async_computation.1 | async-start | bytes 2097152 | tf_op jit(solution)/shard_map/all_to_all | solution.py:26
Sparse Core Ops, SparseCore 0:
  33.6 49.2 all-gather.1
